TPU v7x, 8 devices: a whole 2x2x1 slice. The times are simulated.
8 devices in a mesh: sys: 1 (over z), zdom: 2 (over y), ydom: 4 (over x, core).
Axes of the slice: x: 2, y: 2, z: 1, core: 2. Of those that a mesh axis runs over, the one named last changes fastest.
Arguments:
- charge: float32 [131072], P(('sys', 'ydom', 'zdom'))
- real_mask: int32 [131072], P(('sys', 'ydom', 'zdom'))
- grid_idx: int32 [131072, 3], P(('sys', 'ydom', 'zdom'))
- spline_w: float32 [131072, 3, 4], P(('sys', 'ydom', 'zdom'))
- influence: float32 [96, 96, 96], P(('sys', 'ydom'), 'zdom')
Outputs:
- output 1: float32 [96, 96, 96], P(('sys', 'ydom'), 'zdom')
- output 2: float32 [1], P('sys')
All inputs are finite; a program needn't handle non-finite values.
Results may differ from a plain program's by a relative error of at most 0.001.
Values are sent between devices in bfloat16 or wider.
A program may use at most 1 GiB of HBM per device.

v0:
```python
import functools
import math
import jax
import jax.numpy as jnp
import numpy as np
from jax import lax
from jax.experimental import pallas as pl
from jax.experimental.pallas import tpu as pltpu
from jax.sharding import PartitionSpec as P

MESH = pl.DeviceIdType.MESH
F32 = jnp.float32
BF16 = jnp.bfloat16
G = 96
Y_DEVS = 4
Z_DEVS = 2
LEN_Y = 24
LEN_Z = 48
KX = 24
KY = 48
STEP = 512
GHOST_CHUNK = 2
ROWS = (368, 368, 368, 336)
GHOST_ROW = (320, 320, 320, 288)
WIDTH = (384, 384, 512, 384)
BLOCKS = (12, 12, 15, 12)
Z_SLOT = (0, 12, 36, 24)
Z_SLOTS = 52


def split_np(values):
    high = np.asarray(values, np.float32).astype(jnp.bfloat16)
    low = (np.asarray(values, np.float64) - high.astype(np.float64)).astype(jnp.bfloat16)
    return high, low


def dft_x():
    table = np.zeros((Y_DEVS, 2, KX, 128))
    for dest in range(Y_DEVS):
        angle = 2 * math.pi * (np.outer(np.arange(KX) + KX * dest, np.arange(G)) % G) / G
        table[dest, 0, :, :G] = np.cos(angle)
        table[dest, 1, :, :G] = -np.sin(angle)
    high, low = split_np(table.reshape(Y_DEVS * 2 * KX, 128))
    return np.concatenate([high, high], axis=1), low


def dft_y():
    table = np.zeros((2, Y_DEVS, 32, Z_DEVS, 128))
    for source in range(Y_DEVS):
        y_pos = LEN_Y * source + np.arange(LEN_Y + 3)
        for dest in range(Z_DEVS):
            angle = 2 * math.pi * (np.outer(y_pos, np.arange(KY) + KY * dest) % G) / G
            table[0, source, :LEN_Y + 3, dest, :KY] = np.cos(angle)
            table[1, source, :LEN_Y + 3, dest, :KY] = np.sin(angle)
            table[0, source, :LEN_Y + 3, dest, KY:2 * KY] = -np.sin(angle)
            table[1, source, :LEN_Y + 3, dest, KY:2 * KY] = np.cos(angle)
    return split_np(table.reshape(2 * Y_DEVS * 32, Z_DEVS * 128))


def dft_z():
    table = np.zeros((Z_DEVS, Z_SLOTS, 2, 128))
    for source in range(Z_DEVS):
        for chunk in range(4):
            for block in range(BLOCKS[chunk]):
                z_pos = LEN_Z * source + (4 * block + chunk if block < 12 else LEN_Z + block - 12)
                angle = 2 * math.pi * ((z_pos * np.arange(G)) % G) / G
                table[source, Z_SLOT[chunk] + block, 0, :G] = np.cos(angle)
                table[source, Z_SLOT[chunk] + block, 1, :G] = np.sin(angle)
    return split_np(table.reshape(Z_DEVS * Z_SLOTS, 256))


def split(values):
    high = values.astype(BF16)
    return high, (values - high.astype(F32)).astype(BF16)


def dot(lhs, rhs, lhs_dim, rhs_dim):
    return lax.dot_general(lhs, rhs, (((lhs_dim,), (rhs_dim,)), ((), ())), preferred_element_type=F32)


def kernel(charge, mask, grid_idx, spline_w, influence, fx2, fx_low, fy_high, fy_low, fz_high, fz_low,
           mode_out, energy_out,
           line_x, line_y, tap_z, lhs_a, lhs_b, rhs_a, rhs_b, total, packed, ghosts,
           send0, send1, send2, send3, recv0, recv1, recv2, recv3, half0, half1, half2, half3, zbuf, part, parts,
           y_send_sem, y_recv_sem, z_send_sem, z_recv_sem, e_send_sem, e_recv_sem):
    slots = charge.shape[1]
    me_y = lax.axis_index('ydom')
    me_z = lax.axis_index('zdom')
    me = me_z * Y_DEVS + me_y
    sends, recvs, halves = (send0, send1, send2, send3), (recv0, recv1, recv2, recv3), (half0, half1, half2, half3)

    def device(rank):
        return {'zdom': rank // Y_DEVS, 'ydom': rank % Y_DEVS}

    barrier = pltpu.get_barrier_semaphore()
    for shift in range(1, 8):
        pl.semaphore_signal(barrier, inc=1, device_id=device((me + shift) % 8), device_id_type=MESH)

    row16 = lax.broadcasted_iota(jnp.int32, (16, STEP), 0)
    row96 = lax.broadcasted_iota(jnp.int32, (G, STEP), 0)
    patterns = (row16, jnp.where(row16 < 8, row16 + 16, row16 - 8), row16 + 8, row16 % 4 + 24,
                jnp.where(row16 < 8, row16 + 16, jnp.where(row16 < 12, row16 + 16, 99)))

    def prepare(start):
        at = pl.ds(start, STEP)
        base_x, base_y, base_z = grid_idx[0:1, at], grid_idx[1:2, at], grid_idx[2:3, at]
        weight = charge[0:1, at] * mask[0:1, at].astype(F32)
        values = jnp.zeros((G, STEP), F32)
        for tap in range(4):
            pos = base_x + tap
            pos = jnp.where(pos >= G, pos - G, pos)
            values = jnp.where(row96 == pos, spline_w[0, tap:tap + 1, at] * weight, values)
        line_x[:, at] = values
        for index, pattern in enumerate(patterns):
            values = jnp.zeros((16, STEP), F32)
            offset = pattern - base_y
            for tap in range(4):
                values = jnp.where(offset == tap, spline_w[1, tap:tap + 1, at], values)
            high, low = split(values)
            line_y[index, 0, :, at] = high
            line_y[index, 1, :, at] = low
        for chunk in range(4):
            tap = (chunk - base_z) & 3
            values = jnp.where(tap < 2, jnp.where(tap == 0, spline_w[2, 0:1, at], spline_w[2, 1:2, at]),
                               jnp.where(tap == 2, spline_w[2, 2:3, at], spline_w[2, 3:4, at]))
            tap_z[chunk:chunk + 1, at] = values
            tap_z[4 + chunk:5 + chunk, at] = ((base_z + tap) >> 2).astype(F32)

    def build(chunk, start, lhs, rhs):
        at = pl.ds(start, STEP)
        high, low = split(line_x[:, at] * tap_z[chunk:chunk + 1, at])
        rhs[0:G, :] = high
        rhs[128:128 + G, :] = low
        block = jnp.broadcast_to(tap_z[4 + chunk:5 + chunk, at], (16, STEP))
        block_a = block.astype(BF16)
        block_b = (block - (row16 // 8).astype(F32)).astype(BF16)
        block_g = (block - (row16 // 4).astype(F32)).astype(BF16)
        tiles = []
        for pair in range(6):
            tiles += [(block_a, 2 * pair, 0), (block_b, 2 * pair, 1), (block_a, 2 * pair + 1, 2)]
        if chunk < 3:
            tiles += [(block_a, 12, 0), (block_a, 12, 4)]
        tiles += [(block_g, 0, 3), (block_g, 4, 3), (block_g, 8, 3)]
        zero = jnp.zeros((16, STEP), BF16)
        for index, (source, value, pattern) in enumerate(tiles):
            hit = source == jnp.asarray(value, BF16)
            for half in range(2):
                lhs[half * ROWS[chunk] + 16 * index:half * ROWS[chunk] + 16 * index + 16, :] = jnp.where(
                    hit, line_y[pattern, half, :, at], zero)

    def spread(chunk):
        rows = ROWS[chunk]

        def fill(step, lhs, rhs):
            start = pl.multiple_of(jnp.minimum(step, slots // STEP - 1) * STEP, STEP)
            if chunk == 0:
                prepare(start)
            build(chunk, start, lhs, rhs)

        def add(lhs, rhs):
            product = dot(lhs[0:2 * rows, :], rhs[...], 1, 1)
            total[0:rows, :] += product[:rows] + product[rows:]

        total[...] = jnp.zeros_like(total)
        fill(0, lhs_a, rhs_a)

        def body(pair, carry):
            add(lhs_a, rhs_a)
            fill(2 * pair + 1, lhs_b, rhs_b)
            add(lhs_b, rhs_b)
            fill(2 * pair + 2, lhs_a, rhs_a)
            return carry

        lax.fori_loop(0, slots // STEP // 2, body, 0)

    def transform_x(chunk):
        row8 = lax.broadcasted_iota(jnp.int32, (8, 128), 0)

        def lines(start, count):
            return total[start:start + count, 0:128] + total[start:start + count, 128:256]

        for pair in range(6):
            ghost = lines(GHOST_ROW[chunk] + 8 * pair, 8)
            packed[64 * pair:64 * pair + 24, :] = lines(48 * pair, 24)
            packed[64 * pair + 24:64 * pair + 32, :] = jnp.where(row8 < 4, ghost, 0.0)
            packed[64 * pair + 32:64 * pair + 56, :] = lines(48 * pair + 24, 24)
            packed[64 * pair + 56:64 * pair + 64, :] = jnp.where(row8 < 4, pltpu.roll(ghost, 4, 0), 0.0)
        if chunk < 3:
            ghosts[32 * chunk:32 * chunk + 32, :] = lines(288, 32)
        values = packed[...]
        if chunk == GHOST_CHUNK:
            values = jnp.concatenate([values, ghosts[...]], axis=0)
        high, low = split(values)
        lines_k = dot(fx2[...], jnp.concatenate([high, low], axis=1), 1, 1) + dot(fx_low[...], high, 1, 1)
        for dest in range(Y_DEVS):
            sends[chunk][dest] = lines_k[48 * dest:48 * dest + 48]
        recvs[chunk][me_y] = sends[chunk][me_y]

    def copy_y(chunk, shift):
        dest = (me_y + shift) % Y_DEVS
        return pltpu.make_async_remote_copy(
            src_ref=sends[chunk].at[dest], dst_ref=recvs[chunk].at[me_y],
            send_sem=y_send_sem.at[chunk, shift], recv_sem=y_recv_sem.at[chunk, shift],
            device_id={'ydom': dest}, device_id_type=MESH)

    def start_y(chunk):
        for shift in (2, 1, 3):
            copy_y(chunk, shift).start()

    def wait_y(chunk):
        for shift in (2, 1, 3):
            copy_y(chunk, shift).wait()

    lane = lax.broadcasted_iota(jnp.int32, (KX, 128), 1)

    def regroup(blocks):
        out = list(blocks)
        for first, second in ((0, 2), (1, 3)):
            one, two = out[first], out[second]
            out[first] = jnp.where(lane < 64, one, pltpu.roll(two, 64, 1))
            out[second] = jnp.where(lane < 64, pltpu.roll(one, 64, 1), two)
        for first, second in ((0, 1), (2, 3)):
            one, two = out[first], out[second]
            even = (lane // 32) % 2 == 0
            out[first] = jnp.where(even, one, pltpu.roll(two, 32, 1))
            out[second] = jnp.where(even, pltpu.roll(one, 96, 1), two)
        return out

    def transform_y(chunk):
        recv = recvs[chunk]
        lines_re, lines_im = [], []
        for tile in range(WIDTH[chunk] // 128):
            for part_id, lines in ((0, lines_re), (1, lines_im)):
                lines += regroup([recv[source, KX * part_id:KX * part_id + KX, 128 * tile:128 * tile + 128]
                                  for source in range(Y_DEVS)])
        blocks = BLOCKS[chunk]
        values = jnp.concatenate([jnp.concatenate(lines_re[:blocks], axis=0), jnp.concatenate(lines_im[:blocks], axis=0)], axis=1)
        high, low = split(values)
        lines_k = dot(high, fy_high[...], 1, 0) + dot(high, fy_low[...], 1, 0) + dot(low, fy_high[...], 1, 0)
        first = me_z == 0
        zbuf[me_z, Z_SLOT[chunk] * KX:(Z_SLOT[chunk] + blocks) * KX, :] = jnp.where(first, lines_k[:, :128], lines_k[:, 128:])
        halves[chunk][...] = jnp.where(first, lines_k[:, 128:], lines_k[:, :128])

    def copy_z(chunk):
        return pltpu.make_async_remote_copy(
            src_ref=halves[chunk],
            dst_ref=zbuf.at[me_z, pl.ds(Z_SLOT[chunk] * KX, BLOCKS[chunk] * KX)],
            send_sem=z_send_sem.at[chunk], recv_sem=z_recv_sem.at[chunk],
            device_id={'zdom': 1 - me_z}, device_id_type=MESH)

    rhs_a[...] = jnp.zeros_like(rhs_a)
    rhs_b[...] = jnp.zeros_like(rhs_b)
    ghosts[...] = jnp.zeros_like(ghosts)
    zbuf[:, (Z_SLOTS - 1) * KX:, :] = jnp.zeros((Z_DEVS, KX, 128), F32)

    for chunk in range(4):
        spread(chunk)
        transform_x(chunk)
        if chunk == 0:
            pl.semaphore_wait(barrier, 7)
        start_y(chunk)
        if chunk > 0:
            wait_y(chunk - 1)
            transform_y(chunk - 1)
            copy_z(chunk - 1).start()
    wait_y(3)
    transform_y(3)
    copy_z(3).start()
    for chunk in range(4):
        copy_z(chunk).wait()

    sum_rows = jnp.zeros((8, 128), F32)
    for index in range(KX):
        rows = jnp.concatenate([zbuf[source, pl.ds(index, Z_SLOTS, stride=KX), :] for source in range(Z_DEVS)], axis=0)
        high, low = split(rows)
        lines_k = dot(high, fz_high[...], 0, 0) + dot(high, fz_low[...], 0, 0) + dot(low, fz_high[...], 0, 0)
        real = lines_k[0:KY, 0:G] + lines_k[KY:2 * KY, 128:128 + G]
        imag = lines_k[KY:2 * KY, 0:G] - lines_k[0:KY, 128:128 + G]
        energy = 0.5 * influence[index] * (real * real + imag * imag)
        mode_out[index] = energy
        for row in range(0, KY, 8):
            sum_rows = sum_rows + jnp.pad(energy[row:row + 8], ((0, 0), (0, 128 - G)))
    part[...] = jnp.broadcast_to(jnp.sum(sum_rows), (8, 128))
    parts[me] = part[...]

    def copy_e(shift):
        return pltpu.make_async_remote_copy(
            src_ref=part, dst_ref=parts.at[me], send_sem=e_send_sem.at[shift], recv_sem=e_recv_sem.at[shift],
            device_id=device((me + shift) % 8), device_id_type=MESH)

    for shift in range(1, 8):
        copy_e(shift).start()
    for shift in range(1, 8):
        copy_e(shift).wait()
    result = parts[0]
    for rank in range(1, 8):
        result = result + parts[rank]
    energy_out[...] = result * (1.0 / (G * G * G))


def solution(mesh):
    slot_spec = P(('sys', 'ydom', 'zdom'))
    mode_spec = P(('sys', 'ydom'), 'zdom', None)
    tables = dft_x() + dft_y() + dft_z()

    def local_energy(charge, real_mask, grid_idx, spline_w, influence):
        slots = charge.shape[0]
        vmem = pl.BlockSpec(memory_space=pltpu.VMEM)
        mode_energy, energy = pl.pallas_call(
            kernel,
            out_shape=(jax.ShapeDtypeStruct((KX, KY, G), F32), jax.ShapeDtypeStruct((8, 128), F32)),
            in_specs=[vmem] * 11,
            out_specs=(vmem, vmem),
            scratch_shapes=[
                pltpu.VMEM((G, slots), F32),
                pltpu.VMEM((5, 2, 16, slots), BF16),
                pltpu.VMEM((8, slots), F32),
                pltpu.VMEM((2 * ROWS[0], STEP), BF16),
                pltpu.VMEM((2 * ROWS[0], STEP), BF16),
                pltpu.VMEM((256, STEP), BF16),
                pltpu.VMEM((256, STEP), BF16),
                pltpu.VMEM((ROWS[0], 256), F32),
                pltpu.VMEM((384, 128), F32),
                pltpu.VMEM((128, 128), F32),
            ] + [pltpu.VMEM((Y_DEVS, 2 * KX, width), F32) for width in WIDTH] * 2
            + [pltpu.VMEM((blocks * KX, 128), F32) for blocks in BLOCKS] + [
                pltpu.VMEM((Z_DEVS, Z_SLOTS * KX, 128), F32),
                pltpu.VMEM((8, 128), F32),
                pltpu.VMEM((8, 8, 128), F32),
                pltpu.SemaphoreType.DMA((4, 4)),
                pltpu.SemaphoreType.DMA((4, 4)),
                pltpu.SemaphoreType.DMA((4,)),
                pltpu.SemaphoreType.DMA((4,)),
                pltpu.SemaphoreType.DMA((8,)),
                pltpu.SemaphoreType.DMA((8,)),
            ],
            compiler_params=pltpu.CompilerParams(
                collective_id=0, has_side_effects=True, vmem_limit_bytes=60 * 1024 * 1024),
        )(charge.reshape(1, slots), real_mask.reshape(1, slots), grid_idx.T, jnp.transpose(spline_w, (1, 2, 0)),
          influence, *[jnp.asarray(table) for table in tables])
        return mode_energy, energy[0, 0:1]

    return jax.shard_map(local_energy, mesh=mesh, in_specs=(slot_spec, slot_spec, P(('sys', 'ydom', 'zdom'), None), P(('sys', 'ydom', 'zdom'), None, None), mode_spec), out_specs=(mode_spec, P('sys')), check_vma=False)
```

profile of v0, /device:TPU:0, one launch (start us, length us, event | category | flops | bytes accessed | tf_op | source)
XLA Modules:
  0.0 70.4 jit_solution(8725902863572313717)
XLA Ops:
  0.6 66.7 %shard_map.122 = (f32[24,48,96]{2,1,0:T(8,128)}, f32[8,128]{1,0:T(8,128)}) custom-call(f32[1,16384]{1,0:T(1,128)} %bitcast.7, s32[1,16384]{1,0:T(1,128)} %bitcast.8, s32[3,16384]{1,0:T(4,128)} %bitcast.6, f32[3,4,16384]{2,1,0:T(4,128)} %bitcast.5, f32[24,48,96]{2,1,0:T(8,128)} %influence.1, bf16[192,256]{1,0:T(8,128)(2,1)} %constant.12.clone.fx2, ...), custom_call_target="tpu_custom_call" | custom-call | tf_op jit(solution)/shard_map/pallas_call | solution.py:309
  67.3 1.2 %slice.3 = f32[1,1]{1,0:T(1,128)} slice(f32[8,128]{1,0:T(8,128)} %get-tuple-element.5), slice={[0:1], [0:1]} | slice | bytes 8 | tf_op jit(solution)/shard_map/slice | solution.py:341
  68.5 1.9 %copy.14 = f32[24,48,96]{2,1,0:T(8,128)} copy(f32[24,48,96]{2,1,0:T(8,128)} %get-tuple-element.8) | data formatting | bytes 884736
where the time goes:
time: 70.6 us; the launch traced here: 70.4 us
  Pallas kernels  66.7 us (94%)
  local copies, waits for them, and re-layouts  3.1 us (4%)
    pallas_call x1, Pallas kernels, local_energy(): pl.pallas_call(kernel, out_shape=(jax.ShapeDtypeStruct((KX, KY, G), F32),...  66.7 us
    unnamed x1, local copies, waits for them, and re-layouts  1.92 us

commit v1 on v0

v1 whole, which is shorter than its diff:
```python
import functools
import math
import jax
import jax.numpy as jnp
import numpy as np
from jax import lax
from jax.experimental import pallas as pl
from jax.experimental.pallas import tpu as pltpu
from jax.sharding import PartitionSpec as P

MESH = pl.DeviceIdType.MESH
F32 = jnp.float32
BF16 = jnp.bfloat16
G = 96
Y_DEVS = 4
Z_DEVS = 2
LEN_Y = 24
LEN_Z = 48
KX = 24
KY = 48
STEP = 1024
UNROLL = 8
PART = 1024
PREP = 512
ROWS = (368, 368, 368, 336)
GHOST_ROW = (320, 320, 320, 288)
BLOCKS = (12, 12, 12, 3, 4, 4, 4)
WIDTH = (384, 384, 384, 128, 128, 128, 128)
GHOSTS = 3
LAST = (4, 5, 6)
SLOT = (0, 12, 24, 12, 0, 4, 8)
EARLY = 36
LATE = 16


def split_np(values):
    high = np.asarray(values, np.float32).astype(jnp.bfloat16)
    low = (np.asarray(values, np.float64) - high.astype(np.float64)).astype(jnp.bfloat16)
    return high, low


def dft_x():
    table = np.zeros((Y_DEVS, 2, KX, 128))
    for dest in range(Y_DEVS):
        angle = 2 * math.pi * (np.outer(np.arange(KX) + KX * dest, np.arange(G)) % G) / G
        table[dest, 0, :, :G] = np.cos(angle)
        table[dest, 1, :, :G] = -np.sin(angle)
    high, low = split_np(table.reshape(Y_DEVS * 2 * KX, 128))
    return np.concatenate([high, high], axis=1), low


def dft_y():
    table = np.zeros((2, Y_DEVS, 32, Z_DEVS, 128))
    for source in range(Y_DEVS):
        y_pos = LEN_Y * source + np.arange(LEN_Y + 3)
        for dest in range(Z_DEVS):
            angle = 2 * math.pi * (np.outer(y_pos, np.arange(KY) + KY * dest) % G) / G
            table[0, source, :LEN_Y + 3, dest, :KY] = np.cos(angle)
            table[1, source, :LEN_Y + 3, dest, :KY] = np.sin(angle)
            table[0, source, :LEN_Y + 3, dest, KY:2 * KY] = -np.sin(angle)
            table[1, source, :LEN_Y + 3, dest, KY:2 * KY] = np.cos(angle)
    return split_np(table.reshape(2 * Y_DEVS * 32, Z_DEVS * 128))


def dft_z(messages, slots):
    table = np.zeros((Z_DEVS, slots, 2, 128))
    for source in range(Z_DEVS):
        for message in messages:
            for block in range(BLOCKS[message]):
                if message == GHOSTS:
                    z_pos = LEN_Z + block
                elif message in LAST:
                    z_pos = 4 * (4 * (message - LAST[0]) + block) + 3
                else:
                    z_pos = 4 * block + message
                angle = 2 * math.pi * (((z_pos + LEN_Z * source) * np.arange(G)) % G) / G
                table[source, SLOT[message] + block, 0, :G] = np.cos(angle)
                table[source, SLOT[message] + block, 1, :G] = np.sin(angle)
    return split_np(table.reshape(Z_DEVS * slots, 256))


def split(values):
    high = values.astype(BF16)
    return high, (values - high.astype(F32)).astype(BF16)


def dot(lhs, rhs, lhs_dim, rhs_dim):
    return lax.dot_general(lhs, rhs, (((lhs_dim,), (rhs_dim,)), ((), ())), preferred_element_type=F32)


def kernel(charge, mask, grid_idx, spline_w, influence_in, fx2_in, fx_low_in, fy_high_in, fy_low_in, early_high_in,
           early_low_in, late_in, mode_out, energy_out,
           influence, fx2, fx_low, fy_high, fy_low, early_high, early_low, late, mode,
           line_y, taps, base, lhs_a, lhs_b, rhs_a, rhs_b, total, packed, ghosts, *more):
    slots = charge.shape[1]
    me_y = lax.axis_index('ydom')
    me_z = lax.axis_index('zdom')
    me = me_z * Y_DEVS + me_y
    count = len(BLOCKS)
    sends, recvs, halves = more[:count], more[count:2 * count], more[2 * count:3 * count]
    (z_early, z_late, sums, part, parts,
     y_send_sem, y_recv_sem, z_send_sem, z_recv_sem, e_send_sem, e_recv_sem, in_sem, out_sem) = more[3 * count:]

    loads = [pltpu.make_async_copy(source, dest, in_sem.at[index]) for index, (source, dest) in enumerate((
        (fx2_in, fx2), (fx_low_in, fx_low), (fy_high_in, fy_high), (fy_low_in, fy_low), (early_high_in, early_high),
        (early_low_in, early_low), (late_in, late), (influence_in, influence)))]
    for load in loads:
        load.start()

    def device(rank):
        return {'zdom': rank // Y_DEVS, 'ydom': rank % Y_DEVS}

    barrier = pltpu.get_barrier_semaphore()
    for shift in range(1, 8):
        pl.semaphore_signal(barrier, inc=1, device_id=device((me + shift) % 8), device_id_type=MESH)

    row4 = lax.broadcasted_iota(jnp.int32, (4, PREP), 0)
    row16 = lax.broadcasted_iota(jnp.int32, (16, PART), 0)
    row40 = lax.broadcasted_iota(jnp.int32, (40, PREP), 0)
    row40 = jnp.where(row40 < 32, row40, row40 % 4 + 24)
    row16_f = row16.astype(F32)

    def prepare(start):
        at = pl.ds(start, PREP)
        base_x, base_y, base_z = grid_idx[0:1, at], grid_idx[1:2, at], grid_idx[2:3, at]
        weight = charge[0:1, at] * mask[0:1, at].astype(F32)
        values = jnp.zeros((40, PREP), F32)
        for tap in range(4):
            values = jnp.where(row40 == base_y + tap, spline_w[1, tap:tap + 1, at], values)
        high = values.astype(BF16).astype(F32)
        for half, lines in ((0, high), (1, values - high)):
            for index, (top, bottom) in enumerate(((0, 1), (2, 0), (1, 2), (4, 4), (2, 3))):
                line_y[index, half, :, at] = jnp.concatenate(
                    [lines[8 * top:8 * top + 8], lines[8 * bottom:8 * bottom + 8]], axis=0).astype(BF16)
        tap = (row4 - base_z) & 3
        values = jnp.where(tap < 2, jnp.where(tap == 0, spline_w[2, 0:1, at], spline_w[2, 1:2, at]),
                           jnp.where(tap == 2, spline_w[2, 2:3, at], spline_w[2, 3:4, at]))
        base[0:4, at] = ((base_z + tap) >> 2).astype(F32)
        base[4:5, at] = base_x.astype(F32)
        weight_x = spline_w[0, :, at] * weight
        for chunk in range(4):
            product = weight_x * values[chunk:chunk + 1]
            high = product.astype(BF16).astype(F32)
            taps[chunk, 0:4, at] = high
            taps[chunk, 4:8, at] = product - high

    def build(chunk, start, to, lhs, rhs):
        at = pl.ds(start, PART)

        def spread_row(values):
            return jnp.broadcast_to(values, (16, PART)).astype(BF16)

        base_x = jnp.broadcast_to(base[4:5, at], (16, PART))
        rows = [spread_row(taps[chunk, index:index + 1, at]) for index in range(8)]
        zero = jnp.zeros((16, PART), BF16)
        offset = (row16_f - base_x).astype(BF16)
        wrapped = jnp.where(offset < jnp.asarray(-90, BF16), offset + jnp.asarray(G, BF16), offset)
        for group in range(G // 16):
            high, low = zero, zero
            for tap in range(4):
                hit = (offset if group else wrapped) == jnp.asarray(tap - 16 * group, BF16)
                high = jnp.where(hit, rows[tap], high)
                low = jnp.where(hit, rows[4 + tap], low)
            rhs[16 * group:16 * group + 16, to:to + PART] = high
            rhs[128 + 16 * group:144 + 16 * group, to:to + PART] = low
        block = jnp.broadcast_to(base[chunk:chunk + 1, at], (16, PART))
        block_a = block.astype(BF16)
        block_b = (block - (row16 // 8).astype(F32)).astype(BF16)
        block_g = (block - (row16 // 4).astype(F32)).astype(BF16)
        tiles = []
        for pair in range(6):
            tiles += [(block_a, 2 * pair, 0), (block_b, 2 * pair, 1), (block_a, 2 * pair + 1, 2)]
        if chunk < 3:
            tiles += [(block_a, 12, 0), (block_a, 12, 4)]
        tiles += [(block_g, 0, 3), (block_g, 4, 3), (block_g, 8, 3)]
        for index, (source, value, pattern) in enumerate(tiles):
            hit = source == jnp.asarray(value, BF16)
            for half in range(2):
                lhs[half * ROWS[chunk] + 16 * index:half * ROWS[chunk] + 16 * index + 16, to:to + PART] = jnp.where(
                    hit, line_y[pattern, half, :, at], zero)

    def spread(chunk, first, last):
        rows = ROWS[chunk]

        def fill(step, lhs, rhs):
            start = pl.multiple_of(jnp.minimum(step, slots // STEP - 1) * STEP, STEP)
            for to in range(0, STEP, PART):
                build(chunk, start + to, to, lhs, rhs)

        def add(lhs, rhs):
            product = dot(lhs[0:2 * rows, :], rhs[...], 1, 1)
            total[0:rows, :] += product[:rows] + product[rows:]

        if first == 0:
            total[...] = jnp.zeros_like(total)
            fill(0, lhs_a, rhs_a)

        def body(pair, carry):
            add(lhs_a, rhs_a)
            fill(2 * pair + 1, lhs_b, rhs_b)
            add(lhs_b, rhs_b)
            fill(2 * pair + 2, lhs_a, rhs_a)
            return carry

        lax.fori_loop(first, last, body, 0)

    row8 = lax.broadcasted_iota(jnp.int32, (8, 128), 0)

    def pack(chunk, first, last):
        def lines(start, rows):
            return total[start:start + rows, 0:128] + total[start:start + rows, 128:256]

        for pair in range(first, last):
            ghost = lines(GHOST_ROW[chunk] + 8 * pair, 8)
            packed[64 * pair:64 * pair + 24, :] = lines(48 * pair, 24)
            packed[64 * pair + 24:64 * pair + 32, :] = jnp.where(row8 < 4, ghost, 0.0)
            packed[64 * pair + 32:64 * pair + 56, :] = lines(48 * pair + 24, 24)
            packed[64 * pair + 56:64 * pair + 64, :] = jnp.where(row8 < 4, pltpu.roll(ghost, 4, 0), 0.0)
        if chunk < 3:
            ghosts[32 * chunk:32 * chunk + 32, :] = lines(288, 32)

    def transform_x(message, values):
        high, low = split(values)
        lines_k = dot(fx2[...], jnp.concatenate([high, low], axis=1), 1, 1) + dot(fx_low[...], high, 1, 1)
        for dest in range(Y_DEVS):
            sends[message][dest] = lines_k[48 * dest:48 * dest + 48]
        recvs[message][me_y] = sends[message][me_y]

    def copy_y(chunk, shift):
        dest = (me_y + shift) % Y_DEVS
        return pltpu.make_async_remote_copy(
            src_ref=sends[chunk].at[dest], dst_ref=recvs[chunk].at[me_y],
            send_sem=y_send_sem.at[chunk, shift], recv_sem=y_recv_sem.at[chunk, shift],
            device_id={'ydom': dest}, device_id_type=MESH)

    def start_y(chunk):
        for shift in (2, 1, 3):
            copy_y(chunk, shift).start()

    def wait_y(chunk):
        for shift in (2, 1, 3):
            copy_y(chunk, shift).wait()

    lane = lax.broadcasted_iota(jnp.int32, (KX, 128), 1)

    def regroup(blocks):
        out = list(blocks)
        for first, second in ((0, 2), (1, 3)):
            one, two = out[first], out[second]
            out[first] = jnp.where(lane < 64, one, pltpu.roll(two, 64, 1))
            out[second] = jnp.where(lane < 64, pltpu.roll(one, 64, 1), two)
        for first, second in ((0, 1), (2, 3)):
            one, two = out[first], out[second]
            even = (lane // 32) % 2 == 0
            out[first] = jnp.where(even, one, pltpu.roll(two, 32, 1))
            out[second] = jnp.where(even, pltpu.roll(one, 96, 1), two)
        return out

    def z_rows(message):
        per_source = EARLY if message < GHOSTS else LATE
        return pl.ds((me_z * per_source + SLOT[message]) * KX, BLOCKS[message] * KX)

    def z_buffer(message):
        return z_early if message < GHOSTS else z_late

    def copy_z(message):
        return pltpu.make_async_remote_copy(
            src_ref=halves[message], dst_ref=z_buffer(message).at[z_rows(message)],
            send_sem=z_send_sem.at[message], recv_sem=z_recv_sem.at[message],
            device_id={'zdom': 1 - me_z}, device_id_type=MESH)

    def transform_y(message):
        wait_y(message)
        recv = recvs[message]
        lines_re, lines_im = [], []
        for tile in range(WIDTH[message] // 128):
            for part_id, lines in ((0, lines_re), (1, lines_im)):
                lines += regroup([recv[source, KX * part_id:KX * part_id + KX, 128 * tile:128 * tile + 128]
                                  for source in range(Y_DEVS)])
        blocks = BLOCKS[message]
        values = jnp.concatenate([jnp.concatenate(lines_re[:blocks], axis=0), jnp.concatenate(lines_im[:blocks], axis=0)], axis=1)
        high, low = split(values)
        lines_k = dot(high, fy_high[...], 1, 0) + dot(high, fy_low[...], 1, 0) + dot(low, fy_high[...], 1, 0)
        first = me_z == 0
        halves[message][...] = jnp.where(first, lines_k[:, 128:], lines_k[:, :128])
        z_buffer(message)[z_rows(message), :] = jnp.where(first, lines_k[:, :128], lines_k[:, 128:])
        copy_z(message).start()

    rhs_a[...] = jnp.zeros_like(rhs_a)
    rhs_b[...] = jnp.zeros_like(rhs_b)
    ghosts[...] = jnp.zeros_like(ghosts)
    for source in range(Z_DEVS):
        z_late[((source + 1) * LATE - 1) * KX:(source + 1) * LATE * KX, :] = jnp.zeros((KX, 128), F32)

    def prepare_step(step, carry):
        prepare(pl.multiple_of(step * PREP, PREP))
        return carry

    lax.fori_loop(0, slots // PREP, prepare_step, 0)

    steps = slots // STEP // 2
    for chunk in range(3):
        spread(chunk, 0, steps)
        pack(chunk, 0, 6)
        if chunk == 0:
            for load in loads:
                load.wait()
        transform_x(chunk, packed[...])
        if chunk == 0:
            pl.semaphore_wait(barrier, 7)
        start_y(chunk)
        if chunk == 2:
            transform_x(GHOSTS, ghosts[...])
            start_y(GHOSTS)
        if chunk > 0:
            transform_y(chunk - 1)
    spread(3, 0, steps - 2)
    transform_y(2)
    spread(3, steps - 2, steps)
    for index, message in enumerate(LAST):
        pack(3, 2 * index, 2 * index + 2)
        transform_x(message, packed[128 * index:128 * index + 128, :])
        start_y(message)
    transform_y(GHOSTS)
    for message in range(3):
        copy_z(message).wait()
    def sum_early(index, carry):
        high, low = split(z_early[pl.ds(index, Z_DEVS * EARLY, stride=KX), :])
        high, low = high[:, :2 * KY], low[:, :2 * KY]
        sums[index] = dot(high, early_high[...], 0, 0) + dot(high, early_low[...], 0, 0) + dot(low, early_high[...], 0, 0)
        return carry

    lax.fori_loop(0, KX, sum_early, 0, unroll=UNROLL)
    for message in LAST:
        transform_y(message)
    for message in (GHOSTS,) + LAST:
        copy_z(message).wait()

    def copy_out(index):
        rows = pl.ds(8 * index, 8)
        return pltpu.make_async_copy(mode.at[rows], mode_out.at[rows], out_sem.at[index])

    def sum_late(index, energy_sum):
        high, low = split(z_late[pl.ds(index, Z_DEVS * LATE, stride=KX), :])
        values = jnp.concatenate([high, low, high], axis=0)[:, :2 * KY]
        lines_k = sums[index] + dot(values, late[...], 0, 0)
        real = lines_k[0:KY, 0:G] + lines_k[KY:2 * KY, 128:128 + G]
        imag = lines_k[KY:2 * KY, 0:G] - lines_k[0:KY, 128:128 + G]
        energy = 0.5 * influence[index] * (real * real + imag * imag)
        mode[index] = energy
        return energy_sum + energy

    energy_sum = jnp.zeros((KY, G), F32)
    for index in range(3):
        energy_sum = lax.fori_loop(8 * index, 8 * index + 8, sum_late, energy_sum, unroll=UNROLL)
        copy_out(index).start()
    part[...] = jnp.broadcast_to(jnp.sum(energy_sum), (8, 128))
    parts[me] = part[...]

    def copy_e(shift):
        return pltpu.make_async_remote_copy(
            src_ref=part, dst_ref=parts.at[me], send_sem=e_send_sem.at[shift], recv_sem=e_recv_sem.at[shift],
            device_id=device((me + shift) % 8), device_id_type=MESH)

    for shift in range(1, 8):
        copy_e(shift).start()
    for shift in range(1, 8):
        copy_e(shift).wait()
    result = parts[0]
    for rank in range(1, 8):
        result = result + parts[rank]
    energy_out[...] = result * (1.0 / (G * G * G))
    for index in range(3):
        copy_out(index).wait()


def solution(mesh):
    slot_spec = P(('sys', 'ydom', 'zdom'))
    mode_spec = P(('sys', 'ydom'), 'zdom', None)
    late_high, late_low = dft_z((GHOSTS,) + LAST, LATE)
    tables = dft_x() + dft_y() + dft_z((0, 1, 2), EARLY) + (np.concatenate([late_high, late_high, late_low], axis=0),)

    def local_energy(charge, real_mask, grid_idx, spline_w, influence):
        slots = charge.shape[0]
        vmem = pl.BlockSpec(memory_space=pltpu.VMEM)
        whole = pl.BlockSpec(memory_space=pl.ANY)
        mode_energy, energy = pl.pallas_call(
            kernel,
            out_shape=(jax.ShapeDtypeStruct((KX, KY, G), F32), jax.ShapeDtypeStruct((8, 128), F32)),
            in_specs=[vmem] * 4 + [whole] * (1 + len(tables)),
            out_specs=(whole, vmem),
            scratch_shapes=[
                pltpu.VMEM(influence.shape, F32),
            ] + [pltpu.VMEM(table.shape, BF16) for table in tables] + [
                pltpu.VMEM((KX, KY, G), F32),
                pltpu.VMEM((5, 2, 16, slots), BF16),
                pltpu.VMEM((4, 8, slots), F32),
                pltpu.VMEM((8, slots), F32),
                pltpu.VMEM((2 * ROWS[0], STEP), BF16),
                pltpu.VMEM((2 * ROWS[0], STEP), BF16),
                pltpu.VMEM((256, STEP), BF16),
                pltpu.VMEM((256, STEP), BF16),
                pltpu.VMEM((ROWS[0], 256), F32),
                pltpu.VMEM((384, 128), F32),
                pltpu.VMEM((128, 128), F32),
            ] + [pltpu.VMEM((Y_DEVS, 2 * KX, width), F32) for width in WIDTH] * 2
            + [pltpu.VMEM((blocks * KX, 128), F32) for blocks in BLOCKS] + [
                pltpu.VMEM((Z_DEVS * EARLY * KX, 128), F32),
                pltpu.VMEM((Z_DEVS * LATE * KX, 128), F32),
                pltpu.VMEM((KX, 2 * KY, 256), F32),
                pltpu.VMEM((8, 128), F32),
                pltpu.VMEM((8, 8, 128), F32),
                pltpu.SemaphoreType.DMA((len(BLOCKS), 4)),
                pltpu.SemaphoreType.DMA((len(BLOCKS), 4)),
                pltpu.SemaphoreType.DMA((len(BLOCKS),)),
                pltpu.SemaphoreType.DMA((len(BLOCKS),)),
                pltpu.SemaphoreType.DMA((8,)),
                pltpu.SemaphoreType.DMA((8,)),
                pltpu.SemaphoreType.DMA((8,)),
                pltpu.SemaphoreType.DMA((3,)),
            ],
            compiler_params=pltpu.CompilerParams(
                collective_id=0, has_side_effects=True, vmem_limit_bytes=60 * 1024 * 1024),
        )(charge.reshape(1, slots), real_mask.reshape(1, slots), grid_idx.T, jnp.transpose(spline_w, (1, 2, 0)),
          influence, *[jnp.asarray(table) for table in tables])
        return mode_energy, energy[0, 0:1]

    return jax.shard_map(local_energy, mesh=mesh, in_specs=(slot_spec, slot_spec, P(('sys', 'ydom', 'zdom'), None), P(('sys', 'ydom', 'zdom'), None, None), mode_spec), out_specs=(mode_spec, P('sys')), check_vma=False)
```

time: 70.6 us -> 62.3 us (0.88)
  Pallas kernels: 66.7 us -> 58.3 us
    pallas_call x1, Pallas kernels: 66.7 us -> 58.3 us  [local_energy(): pl.pallas_call(kernel, out_shape=(jax.ShapeDtypeStruct((KX, KY, G), F32),...]
where the time goes in v1:
time: 62.3 us; the launch traced here: 62.1 us
  Pallas kernels  58.3 us (94%)
  local copies, waits for them, and re-layouts  3.1 us (5%)
  between operations  0.64 us (1%)
    pallas_call x1, Pallas kernels, local_energy(): pl.pallas_call(kernel, out_shape=(jax.ShapeDtypeStruct((KX, KY, G), F32),...  58.3 us
    unnamed x1, local copies, waits for them, and re-layouts  1.92 us

profile of v1, /device:TPU:0, one launch (start us, length us, event | category | flops | bytes accessed | tf_op | source)
XLA Modules:
  0.0 62.1 jit_solution(13356119429445860411)
XLA Ops:
  0.6 58.3 %shard_map.131 = (f32[24,48,96]{2,1,0:T(8,128)}, f32[8,128]{1,0:T(8,128)}) custom-call(f32[1,16384]{1,0:T(1,128)} %bitcast.7, s32[1,16384]{1,0:T(1,128)} %bitcast.8, s32[3,16384]{1,0:T(4,128)} %bitcast.6, f32[3,4,16384]{2,1,0:T(4,128)} %bitcast.5, f32[24,48,96]{2,1,0:T(8,128)} %influence_in.1, bf16[192,256]{1,0:T(8,128)(2,1)} %constant.14.clone.fx2_in, ...), custom_call_target="tpu_custom_call" | custom-call | tf_op jit(solution)/shard_map/pallas_call | solution.py:387
  59.0 1.2 %slice.3 = f32[1,1]{1,0:T(1,128)} slice(f32[8,128]{1,0:T(8,128)} %get-tuple-element.5), slice={[0:1], [0:1]} | slice | bytes 8 | tf_op jit(solution)/shard_map/slice | solution.py:426
  60.2 1.9 %copy.15 = f32[24,48,96]{2,1,0:T(8,128)} copy(f32[24,48,96]{2,1,0:T(8,128)} %get-tuple-element.8) | data formatting | bytes 884736

commit v2 on v1

--- a/solution.py
+++ b/solution.py
@@ -18,17 +18,16 @@
 LEN_Z = 48
 KX = 24
 KY = 48
-STEP = 1024
+STEP = 2048
+SECTIONS = 4
 UNROLL = 8
 PART = 1024
 PREP = 512
 ROWS = (368, 368, 368, 336)
 GHOST_ROW = (320, 320, 320, 288)
-BLOCKS = (12, 12, 12, 3, 4, 4, 4)
-WIDTH = (384, 384, 384, 128, 128, 128, 128)
-GHOSTS = 3
-LAST = (4, 5, 6)
-SLOT = (0, 12, 24, 12, 0, 4, 8)
+BLOCKS = (4,) * 12 + (3,)
+GHOSTS = 12
+SLOT = (0, 4, 8, 12, 16, 20, 24, 28, 32, 0, 4, 8, 12)
 EARLY = 36
 LATE = 16
 
@@ -69,10 +68,8 @@
             for block in range(BLOCKS[message]):
                 if message == GHOSTS:
                     z_pos = LEN_Z + block
-                elif message in LAST:
-                    z_pos = 4 * (4 * (message - LAST[0]) + block) + 3
                 else:
-                    z_pos = 4 * block + message
+                    z_pos = 4 * (4 * (message % 3) + block) + message // 3
                 angle = 2 * math.pi * (((z_pos + LEN_Z * source) * np.arange(G)) % G) / G
                 table[source, SLOT[message] + block, 0, :G] = np.cos(angle)
                 table[source, SLOT[message] + block, 1, :G] = np.sin(angle)
@@ -88,9 +85,9 @@
     return lax.dot_general(lhs, rhs, (((lhs_dim,), (rhs_dim,)), ((), ())), preferred_element_type=F32)
 
 
-def kernel(charge, mask, grid_idx, spline_w, influence_in, fx2_in, fx_low_in, fy_high_in, fy_low_in, early_high_in,
-           early_low_in, late_in, mode_out, energy_out,
-           influence, fx2, fx_low, fy_high, fy_low, early_high, early_low, late, mode,
+def kernel(charge_in, mask_in, grid_idx_in, spline_w_in, influence_in, fx2_in, fx_low_in, fy_high_in, fy_low_in, early_high_in,
+           early_low_in, late_in, mode, energy_out,
+           charge, mask, grid_idx, spline_w, influence, fx2, fx_low, fy_high, fy_low, early_high, early_low, late,
            line_y, taps, base, lhs_a, lhs_b, rhs_a, rhs_b, total, packed, ghosts, *more):
     slots = charge.shape[1]
     me_y = lax.axis_index('ydom')
@@ -99,8 +96,17 @@
     count = len(BLOCKS)
     sends, recvs, halves = more[:count], more[count:2 * count], more[2 * count:3 * count]
     (z_early, z_late, sums, part, parts,
-     y_send_sem, y_recv_sem, z_send_sem, z_recv_sem, e_send_sem, e_recv_sem, in_sem, out_sem) = more[3 * count:]
-
+     y_send_sem, y_recv_sem, z_send_sem, z_recv_sem, e_send_sem, e_recv_sem, in_sem, slot_sem) = more[3 * count:]
+
+    def section(index):
+        at = pl.ds(index * (slots // SECTIONS), slots // SECTIONS)
+        return [pltpu.make_async_copy(source.at[..., at], dest.at[..., at], slot_sem.at[index, number])
+                for number, (source, dest) in enumerate((
+                    (charge_in, charge), (mask_in, mask), (grid_idx_in, grid_idx), (spline_w_in, spline_w)))]
+
+    for index in range(SECTIONS):
+        for load in section(index):
+            load.start()
     loads = [pltpu.make_async_copy(source, dest, in_sem.at[index]) for index, (source, dest) in enumerate((
         (fx2_in, fx2), (fx_low_in, fx_low), (fy_high_in, fy_high), (fy_low_in, fy_low), (early_high_in, early_high),
         (early_low_in, early_low), (late_in, late), (influence_in, influence)))]
@@ -219,12 +225,15 @@
         if chunk < 3:
             ghosts[32 * chunk:32 * chunk + 32, :] = lines(288, 32)
 
-    def transform_x(message, values):
+    def transform_x(messages, values):
         high, low = split(values)
         lines_k = dot(fx2[...], jnp.concatenate([high, low], axis=1), 1, 1) + dot(fx_low[...], high, 1, 1)
-        for dest in range(Y_DEVS):
-            sends[message][dest] = lines_k[48 * dest:48 * dest + 48]
-        recvs[message][me_y] = sends[message][me_y]
+        for index, message in enumerate(messages):
+            for dest in range(Y_DEVS):
+                sends[message][dest] = lines_k[48 * dest:48 * dest + 48, 128 * index:128 * index + 128]
+            recvs[message][me_y] = sends[message][me_y]
+        for message in messages:
+            start_y(message)
 
     def copy_y(chunk, shift):
         dest = (me_y + shift) % Y_DEVS
@@ -256,12 +265,15 @@
             out[second] = jnp.where(even, pltpu.roll(one, 96, 1), two)
         return out
 
+    def is_early(message):
+        return message < 9
+
     def z_rows(message):
-        per_source = EARLY if message < GHOSTS else LATE
+        per_source = EARLY if is_early(message) else LATE
         return pl.ds((me_z * per_source + SLOT[message]) * KX, BLOCKS[message] * KX)
 
     def z_buffer(message):
-        return z_early if message < GHOSTS else z_late
+        return z_early if is_early(message) else z_late
 
     def copy_z(message):
         return pltpu.make_async_remote_copy(
@@ -269,22 +281,27 @@
             send_sem=z_send_sem.at[message], recv_sem=z_recv_sem.at[message],
             device_id={'zdom': 1 - me_z}, device_id_type=MESH)
 
-    def transform_y(message):
-        wait_y(message)
-        recv = recvs[message]
+    def transform_y(*messages):
         lines_re, lines_im = [], []
-        for tile in range(WIDTH[message] // 128):
+        for message in messages:
+            wait_y(message)
             for part_id, lines in ((0, lines_re), (1, lines_im)):
-                lines += regroup([recv[source, KX * part_id:KX * part_id + KX, 128 * tile:128 * tile + 128]
-                                  for source in range(Y_DEVS)])
-        blocks = BLOCKS[message]
-        values = jnp.concatenate([jnp.concatenate(lines_re[:blocks], axis=0), jnp.concatenate(lines_im[:blocks], axis=0)], axis=1)
+                lines += regroup([recvs[message][source, KX * part_id:KX * part_id + KX, :]
+                                  for source in range(Y_DEVS)])[:BLOCKS[message]]
+        values = jnp.concatenate([jnp.concatenate(lines_re, axis=0), jnp.concatenate(lines_im, axis=0)], axis=1)
         high, low = split(values)
         lines_k = dot(high, fy_high[...], 1, 0) + dot(high, fy_low[...], 1, 0) + dot(low, fy_high[...], 1, 0)
         first = me_z == 0
-        halves[message][...] = jnp.where(first, lines_k[:, 128:], lines_k[:, :128])
-        z_buffer(message)[z_rows(message), :] = jnp.where(first, lines_k[:, :128], lines_k[:, 128:])
-        copy_z(message).start()
+        there = jnp.where(first, lines_k[:, 128:], lines_k[:, :128])
+        here = jnp.where(first, lines_k[:, :128], lines_k[:, 128:])
+        row = 0
+        for message in messages:
+            rows = BLOCKS[message] * KX
+            halves[message][...] = there[row:row + rows]
+            z_buffer(message)[z_rows(message), :] = here[row:row + rows]
+            row += rows
+        for message in messages:
+            copy_z(message).start()
 
     rhs_a[...] = jnp.zeros_like(rhs_a)
     rhs_b[...] = jnp.zeros_like(rhs_b)
@@ -296,7 +313,11 @@
         prepare(pl.multiple_of(step * PREP, PREP))
         return carry
 
-    lax.fori_loop(0, slots // PREP, prepare_step, 0)
+    part_steps = slots // PREP // SECTIONS
+    for index in range(SECTIONS):
+        for load in section(index):
+            load.wait()
+        lax.fori_loop(index * part_steps, (index + 1) * part_steps, prepare_step, 0)
 
     steps = slots // STEP // 2
     for chunk in range(3):
@@ -305,24 +326,22 @@
         if chunk == 0:
             for load in loads:
                 load.wait()
-        transform_x(chunk, packed[...])
-        if chunk == 0:
             pl.semaphore_wait(barrier, 7)
-        start_y(chunk)
+        transform_x(range(3 * chunk, 3 * chunk + 3), packed[...])
         if chunk == 2:
-            transform_x(GHOSTS, ghosts[...])
-            start_y(GHOSTS)
+            transform_x((GHOSTS,), ghosts[...])
         if chunk > 0:
-            transform_y(chunk - 1)
+            transform_y(*range(3 * chunk - 3, 3 * chunk))
     spread(3, 0, steps - 2)
-    transform_y(2)
-    spread(3, steps - 2, steps)
-    for index, message in enumerate(LAST):
+    transform_y(6)
+    spread(3, steps - 2, steps - 1)
+    transform_y(7)
+    spread(3, steps - 1, steps)
+    for index in range(3):
         pack(3, 2 * index, 2 * index + 2)
-        transform_x(message, packed[128 * index:128 * index + 128, :])
-        start_y(message)
-    transform_y(GHOSTS)
-    for message in range(3):
+        transform_x((9 + index,), packed[128 * index:128 * index + 128, :])
+    transform_y(8, GHOSTS)
+    for message in range(9):
         copy_z(message).wait()
     def sum_early(index, carry):
         high, low = split(z_early[pl.ds(index, Z_DEVS * EARLY, stride=KX), :])
@@ -331,14 +350,10 @@
         return carry
 
     lax.fori_loop(0, KX, sum_early, 0, unroll=UNROLL)
-    for message in LAST:
+    for message in range(9, 12):
         transform_y(message)
-    for message in (GHOSTS,) + LAST:
+    for message in range(9, 13):
         copy_z(message).wait()
-
-    def copy_out(index):
-        rows = pl.ds(8 * index, 8)
-        return pltpu.make_async_copy(mode.at[rows], mode_out.at[rows], out_sem.at[index])
 
     def sum_late(index, energy_sum):
         high, low = split(z_late[pl.ds(index, Z_DEVS * LATE, stride=KX), :])
@@ -353,7 +368,6 @@
     energy_sum = jnp.zeros((KY, G), F32)
     for index in range(3):
         energy_sum = lax.fori_loop(8 * index, 8 * index + 8, sum_late, energy_sum, unroll=UNROLL)
-        copy_out(index).start()
     part[...] = jnp.broadcast_to(jnp.sum(energy_sum), (8, 128))
     parts[me] = part[...]
 
@@ -370,15 +384,13 @@
     for rank in range(1, 8):
         result = result + parts[rank]
     energy_out[...] = result * (1.0 / (G * G * G))
-    for index in range(3):
-        copy_out(index).wait()
 
 
 def solution(mesh):
     slot_spec = P(('sys', 'ydom', 'zdom'))
     mode_spec = P(('sys', 'ydom'), 'zdom', None)
-    late_high, late_low = dft_z((GHOSTS,) + LAST, LATE)
-    tables = dft_x() + dft_y() + dft_z((0, 1, 2), EARLY) + (np.concatenate([late_high, late_high, late_low], axis=0),)
+    late_high, late_low = dft_z(range(9, 13), LATE)
+    tables = dft_x() + dft_y() + dft_z(range(9), EARLY) + (np.concatenate([late_high, late_high, late_low], axis=0),)
 
     def local_energy(charge, real_mask, grid_idx, spline_w, influence):
         slots = charge.shape[0]
@@ -386,13 +398,16 @@
         whole = pl.BlockSpec(memory_space=pl.ANY)
         mode_energy, energy = pl.pallas_call(
             kernel,
-            out_shape=(jax.ShapeDtypeStruct((KX, KY, G), F32), jax.ShapeDtypeStruct((8, 128), F32)),
-            in_specs=[vmem] * 4 + [whole] * (1 + len(tables)),
-            out_specs=(whole, vmem),
+            out_shape=(pltpu.VMEM((KX, KY, G), F32), pltpu.VMEM((8, 128), F32)),
+            in_specs=[whole] * (5 + len(tables)),
+            out_specs=(vmem, vmem),
             scratch_shapes=[
+                pltpu.VMEM((1, slots), F32),
+                pltpu.VMEM((1, slots), jnp.int32),
+                pltpu.VMEM((3, slots), jnp.int32),
+                pltpu.VMEM((3, 4, slots), F32),
                 pltpu.VMEM(influence.shape, F32),
             ] + [pltpu.VMEM(table.shape, BF16) for table in tables] + [
-                pltpu.VMEM((KX, KY, G), F32),
                 pltpu.VMEM((5, 2, 16, slots), BF16),
                 pltpu.VMEM((4, 8, slots), F32),
                 pltpu.VMEM((8, slots), F32),
@@ -403,7 +418,7 @@
                 pltpu.VMEM((ROWS[0], 256), F32),
                 pltpu.VMEM((384, 128), F32),
                 pltpu.VMEM((128, 128), F32),
-            ] + [pltpu.VMEM((Y_DEVS, 2 * KX, width), F32) for width in WIDTH] * 2
+            ] + [pltpu.VMEM((Y_DEVS, 2 * KX, 128), F32) for _ in BLOCKS] * 2
             + [pltpu.VMEM((blocks * KX, 128), F32) for blocks in BLOCKS] + [
                 pltpu.VMEM((Z_DEVS * EARLY * KX, 128), F32),
                 pltpu.VMEM((Z_DEVS * LATE * KX, 128), F32),
@@ -417,7 +432,7 @@
                 pltpu.SemaphoreType.DMA((8,)),
                 pltpu.SemaphoreType.DMA((8,)),
                 pltpu.SemaphoreType.DMA((8,)),
-                pltpu.SemaphoreType.DMA((3,)),
+                pltpu.SemaphoreType.DMA((SECTIONS, 4)),
             ],
             compiler_params=pltpu.CompilerParams(
                 collective_id=0, has_side_effects=True, vmem_limit_bytes=60 * 1024 * 1024),

time: 62.3 us -> 62.1 us (level)
  local copies, waits for them, and re-layouts: 3.1 us -> 1.33 us
  Pallas kernels: 58.3 us -> 59.9 us
    pallas_call x1, Pallas kernels: 58.3 us -> 59.9 us  [local_energy(): pl.pallas_call(kernel, out_shape=(pltpu.VMEM((KX, KY, G), F32), pltpu.VME...]
    unnamed x1, local copies, waits for them, and re-layouts: 1.92 us -> 0.81 us
    slice x1, local copies, waits for them, and re-layouts: 1.19 us -> 0.51 us  [local_energy(): return (mode_energy, energy[0, 0:1])]
where the time goes in v2:
time: 62.1 us; the launch traced here: 61.9 us
  Pallas kernels  59.9 us (96%)
  local copies, waits for them, and re-layouts  1.33 us (2%)
  between operations  0.64 us (1%)
    pallas_call x1, Pallas kernels, local_energy(): pl.pallas_call(kernel, out_shape=(pltpu.VMEM((KX, KY, G), F32), pltpu.VME...  59.9 us

profile of v2, /device:TPU:0, one launch (start us, length us, event | category | flops | bytes accessed | tf_op | source)
XLA Modules:
  0.0 61.9 jit_solution(8059335034930474484)
XLA Ops:
  0.6 59.9 %shard_map.131 = (f32[24,48,96]{2,1,0:T(8,128)S(1)}, f32[8,128]{1,0:T(8,128)S(1)}) custom-call(f32[1,16384]{1,0:T(1,128)} %bitcast.7, s32[1,16384]{1,0:T(1,128)} %bitcast.8, s32[3,16384]{1,0:T(4,128)} %bitcast.6, f32[3,4,16384]{2,1,0:T(4,128)} %bitcast.5, f32[24,48,96]{2,1,0:T(8,128)} %influence_in.1, bf16[192,256]{1,0:T(8,128)(2,1)} %constant.14.clone.fx2_in, ...), custom_call_target="tpu_custom_call" | custom-call | tf_op jit(solution)/shard_map/pallas_call | solution.py:399
  60.5 0.5 slice.3
  61.0 0.8 %copy.15 = f32[24,48,96]{2,1,0:T(8,128)} copy(f32[24,48,96]{2,1,0:T(8,128)S(1)} %get-tuple-element.6) | data formatting | bytes 884736

commit v3 on v1

--- a/solution.py
+++ b/solution.py
@@ -18,7 +18,8 @@
 LEN_Z = 48
 KX = 24
 KY = 48
-STEP = 1024
+STEP = 2048
+SPLIT = 1
 UNROLL = 8
 PART = 1024
 PREP = 512
@@ -89,8 +90,8 @@
 
 
 def kernel(charge, mask, grid_idx, spline_w, influence_in, fx2_in, fx_low_in, fy_high_in, fy_low_in, early_high_in,
-           early_low_in, late_in, mode_out, energy_out,
-           influence, fx2, fx_low, fy_high, fy_low, early_high, early_low, late, mode,
+           early_low_in, late_in, mode, energy_out,
+           influence, fx2, fx_low, fy_high, fy_low, early_high, early_low, late,
            line_y, taps, base, lhs_a, lhs_b, rhs_a, rhs_b, total, packed, ghosts, *more):
     slots = charge.shape[1]
     me_y = lax.axis_index('ydom')
@@ -99,7 +100,7 @@
     count = len(BLOCKS)
     sends, recvs, halves = more[:count], more[count:2 * count], more[2 * count:3 * count]
     (z_early, z_late, sums, part, parts,
-     y_send_sem, y_recv_sem, z_send_sem, z_recv_sem, e_send_sem, e_recv_sem, in_sem, out_sem) = more[3 * count:]
+     y_send_sem, y_recv_sem, z_send_sem, z_recv_sem, e_send_sem, e_recv_sem, in_sem) = more[3 * count:]
 
     loads = [pltpu.make_async_copy(source, dest, in_sem.at[index]) for index, (source, dest) in enumerate((
         (fx2_in, fx2), (fx_low_in, fx_low), (fy_high_in, fy_high), (fy_low_in, fy_low), (early_high_in, early_high),
@@ -314,9 +315,9 @@
             start_y(GHOSTS)
         if chunk > 0:
             transform_y(chunk - 1)
-    spread(3, 0, steps - 2)
+    spread(3, 0, steps - SPLIT)
     transform_y(2)
-    spread(3, steps - 2, steps)
+    spread(3, steps - SPLIT, steps)
     for index, message in enumerate(LAST):
         pack(3, 2 * index, 2 * index + 2)
         transform_x(message, packed[128 * index:128 * index + 128, :])
@@ -336,10 +337,6 @@
     for message in (GHOSTS,) + LAST:
         copy_z(message).wait()
 
-    def copy_out(index):
-        rows = pl.ds(8 * index, 8)
-        return pltpu.make_async_copy(mode.at[rows], mode_out.at[rows], out_sem.at[index])
-
     def sum_late(index, energy_sum):
         high, low = split(z_late[pl.ds(index, Z_DEVS * LATE, stride=KX), :])
         values = jnp.concatenate([high, low, high], axis=0)[:, :2 * KY]
@@ -353,7 +350,6 @@
     energy_sum = jnp.zeros((KY, G), F32)
     for index in range(3):
         energy_sum = lax.fori_loop(8 * index, 8 * index + 8, sum_late, energy_sum, unroll=UNROLL)
-        copy_out(index).start()
     part[...] = jnp.broadcast_to(jnp.sum(energy_sum), (8, 128))
     parts[me] = part[...]
 
@@ -370,8 +366,6 @@
     for rank in range(1, 8):
         result = result + parts[rank]
     energy_out[...] = result * (1.0 / (G * G * G))
-    for index in range(3):
-        copy_out(index).wait()
 
 
 def solution(mesh):
@@ -386,13 +380,12 @@
         whole = pl.BlockSpec(memory_space=pl.ANY)
         mode_energy, energy = pl.pallas_call(
             kernel,
-            out_shape=(jax.ShapeDtypeStruct((KX, KY, G), F32), jax.ShapeDtypeStruct((8, 128), F32)),
+            out_shape=(pltpu.VMEM((KX, KY, G), F32), pltpu.VMEM((8, 128), F32)),
             in_specs=[vmem] * 4 + [whole] * (1 + len(tables)),
-            out_specs=(whole, vmem),
+            out_specs=(vmem, vmem),
             scratch_shapes=[
                 pltpu.VMEM(influence.shape, F32),
             ] + [pltpu.VMEM(table.shape, BF16) for table in tables] + [
-                pltpu.VMEM((KX, KY, G), F32),
                 pltpu.VMEM((5, 2, 16, slots), BF16),
                 pltpu.VMEM((4, 8, slots), F32),
                 pltpu.VMEM((8, slots), F32),
@@ -417,7 +410,6 @@
                 pltpu.SemaphoreType.DMA((8,)),
                 pltpu.SemaphoreType.DMA((8,)),
                 pltpu.SemaphoreType.DMA((8,)),
-                pltpu.SemaphoreType.DMA((3,)),
             ],
             compiler_params=pltpu.CompilerParams(
                 collective_id=0, has_side_effects=True, vmem_limit_bytes=60 * 1024 * 1024),

time: 62.3 us -> 57.5 us (0.923)
  Pallas kernels: 58.3 us -> 55.4 us
  local copies, waits for them, and re-layouts: 3.1 us -> 1.33 us
    pallas_call x1, Pallas kernels: 58.3 us -> 55.4 us  [local_energy(): pl.pallas_call(kernel, out_shape=(pltpu.VMEM((KX, KY, G), F32), pltpu.VME...]
    unnamed x1, local copies, waits for them, and re-layouts: 1.92 us -> 0.81 us
    slice x1, local copies, waits for them, and re-layouts: 1.19 us -> 0.51 us  [local_energy(): return (mode_energy, energy[0, 0:1])]
where the time goes in v3:
time: 57.5 us; the launch traced here: 57.4 us
  Pallas kernels  55.4 us (96%)
  local copies, waits for them, and re-layouts  1.33 us (2%)
  between operations  0.64 us (1%)
    pallas_call x1, Pallas kernels, local_energy(): pl.pallas_call(kernel, out_shape=(pltpu.VMEM((KX, KY, G), F32), pltpu.VME...  55.4 us

profile of v3, /device:TPU:0, one launch (start us, length us, event | category | flops | bytes accessed | tf_op | source)
XLA Modules:
  0.0 57.4 jit_solution(14494623139888395858)
XLA Ops:
  0.6 55.4 %shard_map.131 = (f32[24,48,96]{2,1,0:T(8,128)S(1)}, f32[8,128]{1,0:T(8,128)S(1)}) custom-call(f32[1,16384]{1,0:T(1,128)} %bitcast.7, s32[1,16384]{1,0:T(1,128)} %bitcast.8, s32[3,16384]{1,0:T(4,128)} %bitcast.6, f32[3,4,16384]{2,1,0:T(4,128)} %bitcast.5, f32[24,48,96]{2,1,0:T(8,128)} %influence_in.1, bf16[192,256]{1,0:T(8,128)(2,1)} %constant.14.clone.fx2_in, ...), custom_call_target="tpu_custom_call" | custom-call | tf_op jit(solution)/shard_map/pallas_call | solution.py:381
  56.1 0.5 slice.3
  56.6 0.8 %copy.15 = f32[24,48,96]{2,1,0:T(8,128)} copy(f32[24,48,96]{2,1,0:T(8,128)S(1)} %get-tuple-element.6) | data formatting | bytes 884736

commit v4 on v3

--- a/solution.py
+++ b/solution.py
@@ -24,7 +24,6 @@
 PART = 1024
 PREP = 512
 ROWS = (368, 368, 368, 336)
-GHOST_ROW = (320, 320, 320, 288)
 BLOCKS = (12, 12, 12, 3, 4, 4, 4)
 WIDTH = (384, 384, 384, 128, 128, 128, 128)
 GHOSTS = 3
@@ -136,22 +135,23 @@
         tap = (row4 - base_z) & 3
         values = jnp.where(tap < 2, jnp.where(tap == 0, spline_w[2, 0:1, at], spline_w[2, 1:2, at]),
                            jnp.where(tap == 2, spline_w[2, 2:3, at], spline_w[2, 3:4, at]))
-        base[0:4, at] = ((base_z + tap) >> 2).astype(F32)
-        base[4:5, at] = base_x.astype(F32)
+        block = ((base_z + tap) >> 2).astype(F32)
+        base[:, at] = base_x.astype(F32)
         weight_x = spline_w[0, :, at] * weight
         for chunk in range(4):
             product = weight_x * values[chunk:chunk + 1]
             high = product.astype(BF16).astype(F32)
             taps[chunk, 0:4, at] = high
             taps[chunk, 4:8, at] = product - high
-
-    def build(chunk, start, to, lhs, rhs):
+            taps[chunk, 8:9, at] = block[chunk:chunk + 1]
+
+    def build(chunk, ghosts_too, start, to, lhs, rhs):
         at = pl.ds(start, PART)
 
         def spread_row(values):
             return jnp.broadcast_to(values, (16, PART)).astype(BF16)
 
-        base_x = jnp.broadcast_to(base[4:5, at], (16, PART))
+        base_x = jnp.broadcast_to(base[:, at], (16, PART))
         rows = [spread_row(taps[chunk, index:index + 1, at]) for index in range(8)]
         zero = jnp.zeros((16, PART), BF16)
         offset = (row16_f - base_x).astype(BF16)
@@ -164,37 +164,41 @@
                 low = jnp.where(hit, rows[4 + tap], low)
             rhs[16 * group:16 * group + 16, to:to + PART] = high
             rhs[128 + 16 * group:144 + 16 * group, to:to + PART] = low
-        block = jnp.broadcast_to(base[chunk:chunk + 1, at], (16, PART))
+        block = jnp.broadcast_to(taps[chunk, 8:9, at], (16, PART))
         block_a = block.astype(BF16)
         block_b = (block - (row16 // 8).astype(F32)).astype(BF16)
         block_g = (block - (row16 // 4).astype(F32)).astype(BF16)
         tiles = []
         for pair in range(6):
             tiles += [(block_a, 2 * pair, 0), (block_b, 2 * pair, 1), (block_a, 2 * pair + 1, 2)]
-        if chunk < 3:
+        tiles += [(block_g, 0, 3), (block_g, 4, 3), (block_g, 8, 3)]
+        if ghosts_too:
             tiles += [(block_a, 12, 0), (block_a, 12, 4)]
-        tiles += [(block_g, 0, 3), (block_g, 4, 3), (block_g, 8, 3)]
         for index, (source, value, pattern) in enumerate(tiles):
             hit = source == jnp.asarray(value, BF16)
             for half in range(2):
-                lhs[half * ROWS[chunk] + 16 * index:half * ROWS[chunk] + 16 * index + 16, to:to + PART] = jnp.where(
+                lhs[half * ROWS[0] + 16 * index:half * ROWS[0] + 16 * index + 16, to:to + PART] = jnp.where(
                     hit, line_y[pattern, half, :, at], zero)
 
     def spread(chunk, first, last):
         rows = ROWS[chunk]
 
+        count = slots // STEP
+
         def fill(step, lhs, rhs):
-            start = pl.multiple_of(jnp.minimum(step, slots // STEP - 1) * STEP, STEP)
+            ahead = step // count if chunk < 3 else 0
+            start = pl.multiple_of((step % count) * STEP, STEP)
             for to in range(0, STEP, PART):
-                build(chunk, start + to, to, lhs, rhs)
+                build(chunk + ahead, chunk < 3, start + to, to, lhs, rhs)
 
         def add(lhs, rhs):
-            product = dot(lhs[0:2 * rows, :], rhs[...], 1, 1)
+            product = dot(jnp.concatenate([lhs[0:rows, :], lhs[ROWS[0]:ROWS[0] + rows, :]], axis=0), rhs[...], 1, 1)
             total[0:rows, :] += product[:rows] + product[rows:]
 
         if first == 0:
             total[...] = jnp.zeros_like(total)
-            fill(0, lhs_a, rhs_a)
+            if chunk == 0:
+                fill(0, lhs_a, rhs_a)
 
         def body(pair, carry):
             add(lhs_a, rhs_a)
@@ -212,13 +216,13 @@
             return total[start:start + rows, 0:128] + total[start:start + rows, 128:256]
 
         for pair in range(first, last):
-            ghost = lines(GHOST_ROW[chunk] + 8 * pair, 8)
+            ghost = lines(288 + 8 * pair, 8)
             packed[64 * pair:64 * pair + 24, :] = lines(48 * pair, 24)
             packed[64 * pair + 24:64 * pair + 32, :] = jnp.where(row8 < 4, ghost, 0.0)
             packed[64 * pair + 32:64 * pair + 56, :] = lines(48 * pair + 24, 24)
             packed[64 * pair + 56:64 * pair + 64, :] = jnp.where(row8 < 4, pltpu.roll(ghost, 4, 0), 0.0)
         if chunk < 3:
-            ghosts[32 * chunk:32 * chunk + 32, :] = lines(288, 32)
+            ghosts[32 * chunk:32 * chunk + 32, :] = lines(336, 32)
 
     def transform_x(message, values):
         high, low = split(values)
@@ -271,7 +275,6 @@
             device_id={'zdom': 1 - me_z}, device_id_type=MESH)
 
     def transform_y(message):
-        wait_y(message)
         recv = recvs[message]
         lines_re, lines_im = [], []
         for tile in range(WIDTH[message] // 128):
@@ -285,10 +288,10 @@
         first = me_z == 0
         halves[message][...] = jnp.where(first, lines_k[:, 128:], lines_k[:, :128])
         z_buffer(message)[z_rows(message), :] = jnp.where(first, lines_k[:, :128], lines_k[:, 128:])
-        copy_z(message).start()
-
-    rhs_a[...] = jnp.zeros_like(rhs_a)
-    rhs_b[...] = jnp.zeros_like(rhs_b)
+
+    for rhs in (rhs_a, rhs_b):
+        for row in (G, 128 + G):
+            rhs[row:row + 32, :] = jnp.zeros((32, STEP), BF16)
     ghosts[...] = jnp.zeros_like(ghosts)
     for source in range(Z_DEVS):
         z_late[((source + 1) * LATE - 1) * KX:(source + 1) * LATE * KX, :] = jnp.zeros((KX, 128), F32)
@@ -302,27 +305,35 @@
     steps = slots // STEP // 2
     for chunk in range(3):
         spread(chunk, 0, steps)
-        pack(chunk, 0, 6)
         if chunk == 0:
             for load in loads:
                 load.wait()
+            pl.semaphore_wait(barrier, 7)
+        else:
+            wait_y(chunk - 1)
+        pack(chunk, 0, 6)
         transform_x(chunk, packed[...])
-        if chunk == 0:
-            pl.semaphore_wait(barrier, 7)
+        if chunk == 2:
+            transform_x(GHOSTS, ghosts[...])
+        if chunk > 0:
+            transform_y(chunk - 1)
         start_y(chunk)
         if chunk == 2:
-            transform_x(GHOSTS, ghosts[...])
             start_y(GHOSTS)
         if chunk > 0:
-            transform_y(chunk - 1)
+            copy_z(chunk - 1).start()
     spread(3, 0, steps - SPLIT)
+    wait_y(2)
     transform_y(2)
+    copy_z(2).start()
     spread(3, steps - SPLIT, steps)
     for index, message in enumerate(LAST):
         pack(3, 2 * index, 2 * index + 2)
         transform_x(message, packed[128 * index:128 * index + 128, :])
         start_y(message)
+    wait_y(GHOSTS)
     transform_y(GHOSTS)
+    copy_z(GHOSTS).start()
     for message in range(3):
         copy_z(message).wait()
     def sum_early(index, carry):
@@ -333,7 +344,9 @@
 
     lax.fori_loop(0, KX, sum_early, 0, unroll=UNROLL)
     for message in LAST:
+        wait_y(message)
         transform_y(message)
+        copy_z(message).start()
     for message in (GHOSTS,) + LAST:
         copy_z(message).wait()
 
@@ -387,8 +400,8 @@
                 pltpu.VMEM(influence.shape, F32),
             ] + [pltpu.VMEM(table.shape, BF16) for table in tables] + [
                 pltpu.VMEM((5, 2, 16, slots), BF16),
-                pltpu.VMEM((4, 8, slots), F32),
-                pltpu.VMEM((8, slots), F32),
+                pltpu.VMEM((4, 9, slots), F32),
+                pltpu.VMEM((1, slots), F32),
                 pltpu.VMEM((2 * ROWS[0], STEP), BF16),
                 pltpu.VMEM((2 * ROWS[0], STEP), BF16),
                 pltpu.VMEM((256, STEP), BF16),

time: 57.5 us -> 55.3 us (0.962)
  Pallas kernels: 55.4 us -> 53.2 us
    pallas_call x1, Pallas kernels: 55.4 us -> 53.2 us  [local_energy(): pl.pallas_call(kernel, out_shape=(pltpu.VMEM((KX, KY, G), F32), pltpu.VME...]
where the time goes in v4:
time: 55.3 us; the launch traced here: 55.2 us
  Pallas kernels  53.2 us (96%)
  local copies, waits for them, and re-layouts  1.33 us (2%)
  between operations  0.64 us (1%)
    pallas_call x1, Pallas kernels, local_energy(): pl.pallas_call(kernel, out_shape=(pltpu.VMEM((KX, KY, G), F32), pltpu.VME...  53.2 us

profile of v4, /device:TPU:0, one launch (start us, length us, event | category | flops | bytes accessed | tf_op | source)
XLA Modules:
  0.0 55.2 jit_solution(9570887795521523736)
XLA Ops:
  0.6 53.2 %shard_map.131 = (f32[24,48,96]{2,1,0:T(8,128)S(1)}, f32[8,128]{1,0:T(8,128)S(1)}) custom-call(f32[1,16384]{1,0:T(1,128)} %bitcast.7, s32[1,16384]{1,0:T(1,128)} %bitcast.8, s32[3,16384]{1,0:T(4,128)} %bitcast.6, f32[3,4,16384]{2,1,0:T(4,128)} %bitcast.5, f32[24,48,96]{2,1,0:T(8,128)} %influence_in.1, bf16[192,256]{1,0:T(8,128)(2,1)} %constant.14.clone.fx2_in, ...), custom_call_target="tpu_custom_call" | custom-call | tf_op jit(solution)/shard_map/pallas_call | solution.py:394
  53.8 0.5 slice.3
  54.4 0.8 %copy.15 = f32[24,48,96]{2,1,0:T(8,128)} copy(f32[24,48,96]{2,1,0:T(8,128)S(1)} %get-tuple-element.6) | data formatting | bytes 884736

commit v5 on v4

--- a/solution.py
+++ b/solution.py
@@ -20,7 +20,7 @@
 KY = 48
 STEP = 2048
 SPLIT = 1
-UNROLL = 8
+UNROLL = 6
 PART = 1024
 PREP = 512
 ROWS = (368, 368, 368, 336)
@@ -334,19 +334,22 @@
     wait_y(GHOSTS)
     transform_y(GHOSTS)
     copy_z(GHOSTS).start()
-    for message in range(3):
-        copy_z(message).wait()
     def sum_early(index, carry):
         high, low = split(z_early[pl.ds(index, Z_DEVS * EARLY, stride=KX), :])
         high, low = high[:, :2 * KY], low[:, :2 * KY]
         sums[index] = dot(high, early_high[...], 0, 0) + dot(high, early_low[...], 0, 0) + dot(low, early_high[...], 0, 0)
         return carry
 
-    lax.fori_loop(0, KX, sum_early, 0, unroll=UNROLL)
-    for message in LAST:
+    for index, message in enumerate(LAST):
         wait_y(message)
         transform_y(message)
         copy_z(message).start()
+        if index == 0:
+            for early in range(3):
+                copy_z(early).wait()
+            lax.fori_loop(0, KX // 2, sum_early, 0, unroll=UNROLL)
+        elif index == 1:
+            lax.fori_loop(KX // 2, KX, sum_early, 0, unroll=UNROLL)
     for message in (GHOSTS,) + LAST:
         copy_z(message).wait()
 
@@ -362,7 +365,7 @@
 
     energy_sum = jnp.zeros((KY, G), F32)
     for index in range(3):
-        energy_sum = lax.fori_loop(8 * index, 8 * index + 8, sum_late, energy_sum, unroll=UNROLL)
+        energy_sum = lax.fori_loop(8 * index, 8 * index + 8, sum_late, energy_sum, unroll=8)
     part[...] = jnp.broadcast_to(jnp.sum(energy_sum), (8, 128))
     parts[me] = part[...]
 

time: 55.3 us -> 55.1 us (level)
  no operation moved by 1% of the time
where the time goes in v5:
time: 55.1 us; the launch traced here: 55 us
  Pallas kernels  53 us (96%)
  local copies, waits for them, and re-layouts  1.33 us (2%)
  between operations  0.64 us (1%)
    pallas_call x1, Pallas kernels, local_energy(): pl.pallas_call(kernel, out_shape=(pltpu.VMEM((KX, KY, G), F32), pltpu.VME...  53 us

profile of v5, /device:TPU:0, one launch (start us, length us, event | category | flops | bytes accessed | tf_op | source)
XLA Modules:
  0.0 55.0 jit_solution(9194811041650447853)
XLA Ops:
  0.6 53.0 %shard_map.131 = (f32[24,48,96]{2,1,0:T(8,128)S(1)}, f32[8,128]{1,0:T(8,128)S(1)}) custom-call(f32[1,16384]{1,0:T(1,128)} %bitcast.7, s32[1,16384]{1,0:T(1,128)} %bitcast.8, s32[3,16384]{1,0:T(4,128)} %bitcast.6, f32[3,4,16384]{2,1,0:T(4,128)} %bitcast.5, f32[24,48,96]{2,1,0:T(8,128)} %influence_in.1, bf16[192,256]{1,0:T(8,128)(2,1)} %constant.14.clone.fx2_in, ...), custom_call_target="tpu_custom_call" | custom-call | tf_op jit(solution)/shard_map/pallas_call | solution.py:397
  53.7 0.5 slice.3
  54.2 0.8 %copy.15 = f32[24,48,96]{2,1,0:T(8,128)} copy(f32[24,48,96]{2,1,0:T(8,128)S(1)} %get-tuple-element.6) | data formatting | bytes 884736

commit v6 on v5

--- a/solution.py
+++ b/solution.py
@@ -20,6 +20,7 @@
 KY = 48
 STEP = 2048
 SPLIT = 1
+SECTIONS = 2
 UNROLL = 6
 PART = 1024
 PREP = 512
@@ -88,19 +89,28 @@
     return lax.dot_general(lhs, rhs, (((lhs_dim,), (rhs_dim,)), ((), ())), preferred_element_type=F32)
 
 
-def kernel(charge, mask, grid_idx, spline_w, influence_in, fx2_in, fx_low_in, fy_high_in, fy_low_in, early_high_in,
+def kernel(charge_in, mask_in, grid_idx_in, spline_w_in, influence_in, fx2_in, fx_low_in, fy_high_in, fy_low_in, early_high_in,
            early_low_in, late_in, mode, energy_out,
-           influence, fx2, fx_low, fy_high, fy_low, early_high, early_low, late,
+           charge, mask, grid_idx, spline_w, influence, fx2, fx_low, fy_high, fy_low, early_high, early_low, late,
            line_y, taps, base, lhs_a, lhs_b, rhs_a, rhs_b, total, packed, ghosts, *more):
-    slots = charge.shape[1]
+    slots = charge_in.shape[1]
     me_y = lax.axis_index('ydom')
     me_z = lax.axis_index('zdom')
     me = me_z * Y_DEVS + me_y
     count = len(BLOCKS)
     sends, recvs, halves = more[:count], more[count:2 * count], more[2 * count:3 * count]
     (z_early, z_late, sums, part, parts,
-     y_send_sem, y_recv_sem, z_send_sem, z_recv_sem, e_send_sem, e_recv_sem, in_sem) = more[3 * count:]
-
+     y_send_sem, y_recv_sem, z_send_sem, z_recv_sem, e_send_sem, e_recv_sem, in_sem, slot_sem) = more[3 * count:]
+
+    def section(index):
+        at = pl.ds(index * (slots // SECTIONS), slots // SECTIONS)
+        return [pltpu.make_async_copy(source.at[..., at], dest.at[..., at], slot_sem.at[index, number])
+                for number, (source, dest) in enumerate((
+                    (charge_in, charge), (mask_in, mask), (grid_idx_in, grid_idx), (spline_w_in, spline_w)))]
+
+    for index in range(SECTIONS):
+        for load in section(index):
+            load.start()
     loads = [pltpu.make_async_copy(source, dest, in_sem.at[index]) for index, (source, dest) in enumerate((
         (fx2_in, fx2), (fx_low_in, fx_low), (fy_high_in, fy_high), (fy_low_in, fy_low), (early_high_in, early_high),
         (early_low_in, early_low), (late_in, late), (influence_in, influence)))]
@@ -300,7 +310,11 @@
         prepare(pl.multiple_of(step * PREP, PREP))
         return carry
 
-    lax.fori_loop(0, slots // PREP, prepare_step, 0)
+    part_steps = slots // PREP // SECTIONS
+    for index in range(SECTIONS):
+        for load in section(index):
+            load.wait()
+        lax.fori_loop(index * part_steps, (index + 1) * part_steps, prepare_step, 0)
 
     steps = slots // STEP // 2
     for chunk in range(3):
@@ -397,9 +411,13 @@
         mode_energy, energy = pl.pallas_call(
             kernel,
             out_shape=(pltpu.VMEM((KX, KY, G), F32), pltpu.VMEM((8, 128), F32)),
-            in_specs=[vmem] * 4 + [whole] * (1 + len(tables)),
+            in_specs=[whole] * (5 + len(tables)),
             out_specs=(vmem, vmem),
             scratch_shapes=[
+                pltpu.VMEM((1, slots), F32),
+                pltpu.VMEM((1, slots), jnp.int32),
+                pltpu.VMEM((3, slots), jnp.int32),
+                pltpu.VMEM((3, 4, slots), F32),
                 pltpu.VMEM(influence.shape, F32),
             ] + [pltpu.VMEM(table.shape, BF16) for table in tables] + [
                 pltpu.VMEM((5, 2, 16, slots), BF16),
@@ -426,6 +444,7 @@
                 pltpu.SemaphoreType.DMA((8,)),
                 pltpu.SemaphoreType.DMA((8,)),
                 pltpu.SemaphoreType.DMA((8,)),
+                pltpu.SemaphoreType.DMA((SECTIONS, 4)),
             ],
             compiler_params=pltpu.CompilerParams(
                 collective_id=0, has_side_effects=True, vmem_limit_bytes=60 * 1024 * 1024),

time: 55.1 us -> 55.1 us (level)
  no operation moved by 1% of the time
where the time goes in v6:
time: 55.1 us; the launch traced here: 55 us
  Pallas kernels  53 us (96%)
  local copies, waits for them, and re-layouts  1.33 us (2%)
  between operations  0.64 us (1%)
    pallas_call x1, Pallas kernels, local_energy(): pl.pallas_call(kernel, out_shape=(pltpu.VMEM((KX, KY, G), F32), pltpu.VME...  53 us

profile of v6, /device:TPU:0, one launch (start us, length us, event | category | flops | bytes accessed | tf_op | source)
XLA Modules:
  0.0 55.0 jit_solution(4988410473173203171)
XLA Ops:
  0.6 53.0 %shard_map.131 = (f32[24,48,96]{2,1,0:T(8,128)S(1)}, f32[8,128]{1,0:T(8,128)S(1)}) custom-call(f32[1,16384]{1,0:T(1,128)} %bitcast.7, s32[1,16384]{1,0:T(1,128)} %bitcast.8, s32[3,16384]{1,0:T(4,128)} %bitcast.6, f32[3,4,16384]{2,1,0:T(4,128)} %bitcast.5, f32[24,48,96]{2,1,0:T(8,128)} %influence_in.1, bf16[192,256]{1,0:T(8,128)(2,1)} %constant.14.clone.fx2_in, ...), custom_call_target="tpu_custom_call" | custom-call | tf_op jit(solution)/shard_map/pallas_call | solution.py:411
  53.7 0.5 slice.3
  54.2 0.8 %copy.15 = f32[24,48,96]{2,1,0:T(8,128)} copy(f32[24,48,96]{2,1,0:T(8,128)S(1)} %get-tuple-element.6) | data formatting | bytes 884736
